TPU v7x, 32 devices: a whole 2x2x4 slice. The times are simulated.
32 devices in a mesh: shot: 4 (over y, core), space: 8 (over z, x).
Axes of the slice: x: 2, y: 2, z: 4, core: 2. Of those that a mesh axis runs over, the one named last changes fastest.
Arguments:
- adjoint_now: float32 [4, 128, 64, 512], P('shot', 'space'), may hold values from -6 to 6
- adjoint_later: float32 [4, 128, 64, 512], P('shot', 'space'), may hold values from -6 to 6
- courant: float32 [128, 64, 512], P('space'), may hold values from 0.05 to 0.2
- checkpoint_codes: int32 [4, 6, 128, 64, 128], P('shot', None, 'space'), may hold values from -2147483648 to 2147483646
- scale_index: int32 [4, 6, 128, 256], P('shot', None, 'space'), may hold values from 0 to 63
- scale_table: float32 [64], replicated, may hold values from 0.001 to 0.01
- receiver_cell: int32 [4, 2048], P('shot', 'space'), may hold values from 0 to 4194303, as said below
- observed: float32 [4, 4, 2048], P('shot', None, 'space'), may hold values from -12 to 12
- source_cell: int32 [4, 3], P('shot'), may hold values from 0 to 511, as said below
Outputs:
- gradient: float32 [128, 64, 512], P('space', 'shot')
- adjoint_first: float32 [4, 128, 64, 512], P('shot', 'space')
- adjoint_second: float32 [4, 128, 64, 512], P('shot', 'space')
- misfit: float32 [], replicated
Inputs may be any that keep to these rules, and one draw needn't show every extreme that they name: `receiver_cell`: for every r, entries r * 256 to (r + 1) * 256 - 1 of each shot's row are flat indices (z * 64 + y) * 512 + x of cells with r * 16 <= z < (r + 1) * 16. `source_cell`: column 0 is a z index below 128, column 1 a y index below 64, column 2 an x index below 512.
All inputs are finite; a program needn't handle non-finite values.
Results may differ from a plain program's by a relative error of at most 0.0001.
Values sent between devices are 32-bit elements; how exact they have to be, the bound alone decides.
A program may use at most 128 MiB of HBM per device.

v0:
```python
import jax
import jax.numpy as jnp
from jax import lax
from jax.sharding import PartitionSpec as P

ITERS = 4
QBLOCK = 128
MUTE = 8


COEFFS = (-205.0 / 72.0, 8.0 / 5.0, -1.0 / 5.0, 8.0 / 315.0, -1.0 / 560.0)


def with_halo(block, sides, width):
    for axis, dim in sides:
        count = lax.axis_size(axis)
        forward = [(i, i + 1) for i in range(count - 1)]
        backward = [(target, source) for source, target in forward]
        low = lax.ppermute(
            lax.slice_in_dim(block, block.shape[dim] - width, None, axis=dim), axis, forward
        )
        high = lax.ppermute(lax.slice_in_dim(block, 0, width, axis=dim), axis, backward)
        block = jnp.concatenate([low, block, high], axis=dim)
    return block


def decode(words, index, table):
    planes = [jnp.bitwise_and(jnp.right_shift(words, 8 * m), 255) for m in range(4)]
    codes = jnp.concatenate(planes, axis=-1)
    centred = (codes - 128).astype(jnp.float32)
    depth, rows, cols = centred.shape
    onehot = index[..., None] == jnp.arange(table.shape[0], dtype=jnp.int32)
    scale = jnp.sum(jnp.where(onehot, table, 0.0), axis=-1)
    blocks = centred.reshape(depth, rows, cols // QBLOCK, QBLOCK) * scale.reshape(
        depth, rows, cols // QBLOCK, 1
    )
    return blocks.reshape(depth, rows, cols)


def laplace(field):
    depth, rows, cols = field.shape
    deep = with_halo(field, (("space", 0),), 4)
    flat = jnp.pad(field, ((0, 0), (4, 4), (4, 4)))
    total = 3.0 * COEFFS[0] * field
    for step in range(1, 5):
        total = total + COEFFS[step] * (
            deep[4 + step : 4 + step + depth] + deep[4 - step : 4 - step + depth]
        )
        total = total + COEFFS[step] * (
            flat[:, 4 + step : 4 + step + rows, 4 : 4 + cols]
            + flat[:, 4 - step : 4 - step + rows, 4 : 4 + cols]
        )
        total = total + COEFFS[step] * (
            flat[:, 4 : 4 + rows, 4 + step : 4 + step + cols]
            + flat[:, 4 : 4 + rows, 4 - step : 4 - step + cols]
        )
    return total


def body(
    adjoint_now,
    adjoint_later,
    courant,
    checkpoint_codes,
    scale_index,
    scale_table,
    receiver_cell,
    observed,
    source_cell,
):
    now = adjoint_now[0]
    later = adjoint_later[0]
    depth, rows, cols = now.shape
    first_z = lax.axis_index("space") * depth
    cells = receiver_cell[0] - first_z * (rows * cols)
    fields = [
        decode(checkpoint_codes[0, level], scale_index[0, level], scale_table)
        for level in range(ITERS + 2)
    ]
    image = jnp.zeros((depth, rows, cols), jnp.float32)
    misfit_part = jnp.zeros((), jnp.float32)
    for step in range(ITERS):
        level = ITERS - step
        synthetic = jnp.take(fields[level].reshape(-1), cells)
        residual = synthetic - observed[0, level - 1]
        misfit_part = misfit_part + jnp.sum(residual * residual)
        image = image + now * (fields[level + 1] - 2.0 * fields[level] + fields[level - 1])
        stepped = 2.0 * now - later + courant * laplace(now)
        stepped = stepped.reshape(-1).at[cells].add(residual).reshape(depth, rows, cols)
        later = now
        now = stepped
    source = source_cell[0]
    zpos = (first_z + jnp.arange(depth, dtype=jnp.int32)).reshape(depth, 1, 1)
    ypos = jnp.arange(rows, dtype=jnp.int32).reshape(1, rows, 1)
    xpos = jnp.arange(cols, dtype=jnp.int32).reshape(1, 1, cols)
    dist = ((zpos - source[0]) ** 2 + (ypos - source[1]) ** 2 + (xpos - source[2]) ** 2).astype(
        jnp.float32
    )
    muted = image * (1.0 - jnp.exp(-dist / (2.0 * MUTE * MUTE)))
    gradient = lax.psum_scatter(muted, "shot", scatter_dimension=1, tiled=True)
    count = lax.axis_size("shot") * ITERS * receiver_cell.shape[1] * lax.axis_size("space")
    misfit = 0.5 * lax.psum(misfit_part, ("shot", "space")) / count
    return (gradient, now[None], later[None], misfit)


def solution(mesh):
    placed = (
        P("shot", "space", None, None),
        P("shot", "space", None, None),
        P("space", None, None),
        P("shot", None, "space", None, None),
        P("shot", None, "space", None),
        P(),
        P("shot", "space"),
        P("shot", None, "space"),
        P("shot", None),
    )
    return jax.shard_map(
        body,
        mesh=mesh,
        in_specs=placed,
        out_specs=(
            P("space", "shot", None),
            P("shot", "space", None, None),
            P("shot", "space", None, None),
            P(),
        ),
        check_vma=False,
    )
```

profile of v0, /device:TPU:2, one launch (start us, length us, event | category | flops | bytes accessed | tf_op | source)
XLA Modules:
  0.0 307.7 jit_solution(9114764034815318383)
XLA Ops:
  11.4 4.8 %collective-permute-start.1 = (f32[4,64,512]{2,1,0:T(8,128)}, f32[4,64,512]{2,1,0:T(8,128)}, u32[]{:S(2)}, u32[]{:S(2)}) collective-permute-start(f32[4,64,512]{2,1,0:T(8,128)} %get-tuple-element.59), channel_id=1, source_target_pairs={{0,1},{1,2},{2,3},{3,4},{4,5},{5,6},{6,7},{8,9},{9,10},{10,11},{11... | collective-permute-start | bytes 1572872 | tf_op jit(solution)/shard_map/ppermute | solution.py:19
  16.2 3.3 %and_bitcast_fusion.7 = (s32[16,64,1,128]{3,1,0,2:T(8,128)}, s32[16,64,1,128]{3,1,0,2:T(8,128)}, s32[16,64,1,128]{3,1,0,2:T(8,128)}, s32[16,64,1,128]{3,1,0,2:T(8,128)}, s32[16,64,1,128]{3,1,0,2:T(8,128)S(1)}) fusion(s32[1,6,16,64,128]{4,3,2,1,0:T(8,128)} %param.14), kind=kLoop, calls=%fused_computation.304 | loop fusion | flops 1310720 | bytes 5242880 | tf_op jit(solution)/shard_map/and | solution.py:28
  19.6 3.7 %and_bitcast_fusion.23 = (s32[16,64,1,128]{3,1,0,2:T(8,128)S(1)}, s32[16,64,1,128]{3,1,0,2:T(8,128)}, s32[16,64,1,128]{3,1,0,2:T(8,128)}, s32[16,64,1,128]{3,1,0...) fusion(s32[1,6,16,64,128]{4,3,2,1,0:T(8,128)S(1)} %copy-done.11), kind=kLoop, calls=%fused_computation.322 | loop fusion | flops 4980736 | bytes 13107200 | tf_op jit(solution)/shard_map/and | solution.py:28
  25.6 3.9 %fusion.162 = (f32[16,64,4,128]{3,1,0,2:T(8,128)S(1)}, f32[16,64,4,128]{3,1,0,2:T(8,128)S(1)}) fusion(s32[16,64,1,128]{3,1,0,2:T(8,128)} %get-tuple-element.27, s32[16,64,1,128]{3,1,0,2:T(8,128)} %get-tuple-element.26, s32[16,64,1,128]{3,1,0,2:T(8,128)} %get-tuple-element.25, s32[16,64,1,128]{3,1,0,2:T(8,128)} %get-tuple-element.43, ...), kind=kLoop, calls=%fused_computation.270 | loop fusion | flops 6291456 | bytes 8421376 | tf_op jit(solution)/shard_map/mul | solution.py:34
  37.8 3.4 %gather_fusion = f32[256]{0:T(256)S(1)} fusion(f32[524288]{0:T(1024)} %bitcast.181, s32[1024]{0:T(1024)S(1)} %pad_clamp_fusion), kind=kCustom, calls=%fused_computation.clone | custom fusion | bytes 3072 | tf_op jit(solution)/shard_map/jit(_take)/gather | solution.py:84
  41.2 3.5 %gather_fusion.1 = f32[256]{0:T(256)S(1)} fusion(f32[524288]{0:T(1024)} %bitcast.182, s32[1024]{0:T(1024)S(1)} %pad_clamp_fusion), kind=kCustom, calls=%fused_computation.1.clone | custom fusion | bytes 3072 | tf_op jit(solution)/shard_map/jit(_take)/gather | solution.py:84
  47.4 3.5 %gather_fusion.2 = f32[256]{0:T(256)S(1)} fusion(f32[524288]{0:T(1024)} %bitcast.184, s32[1024]{0:T(1024)S(1)} %pad_clamp_fusion), kind=kCustom, calls=%fused_computation.2.clone | custom fusion | bytes 3072 | tf_op jit(solution)/shard_map/jit(_take)/gather | solution.py:84
  50.9 4.5 %copy.51 = f32[16,64,4,128]{3,2,1,0:T(4,128)} copy(f32[16,64,4,128]{3,1,0,2:T(8,128)} %get-tuple-element.84) | data formatting | bytes 4194304 | tf_op jit(solution)/shard_map/mul | solution.py:34
  55.3 3.5 %gather_fusion.3 = f32[256]{0:T(256)S(1)} fusion(f32[524288]{0:T(1024)} %bitcast.183, s32[1024]{0:T(1024)S(1)} %pad_clamp_fusion), kind=kCustom, calls=%fused_computation.3.clone | custom fusion | bytes 3072 | tf_op jit(solution)/shard_map/jit(_take)/gather | solution.py:84
  59.5 29.2 %fusion.10 = f32[16,64,512]{2,1,0:T(8,128)S(1)} fusion(f32[16,64,512]{2,1,0:T(8,128)S(1)} %copy-done.2, f32[16,64,512]{2,1,0:T(8,128)} %bitcast.173, f32[4,64,512]{2,1,0:T(8,128)} %collective-permute-done.1, f32[4,64,512]{2,1,0:T(8,128)} %collective-permute-done, f32[1,16,64,512]{3,2,1,0:T(8,128)} %param.12), kind=kLoop, calls=%fused_computation.94 | loop fusion | flops 25690112 | bytes 9437184 | tf_op jit(solution)/shard_map/add | solution.py:88
  89.3 2.9 scatter_fusion
  99.8 4.1 %collective-permute-start.2 = (f32[4,64,512]{2,1,0:T(8,128)}, f32[4,64,512]{2,1,0:T(8,128)}, u32[]{:S(2)}, u32[]{:S(2)}) collective-permute-start(f32[4,64,512]{2,1,0:T(8,128)} %slice.514), channel_id=1, source_target_pairs={{1,0},{2,1},{3,2},{4,3},{5,4},{6,5},{7,6},{9,8},{10,9},{11,10},{12... | collective-permute-start | bytes 1572872 | tf_op jit(solution)/shard_map/ppermute | solution.py:22
  105.6 16.2 %collective-permute-done.3 = f32[4,64,512]{2,1,0:T(8,128)} collective-permute-done((f32[4,64,512]{2,1,0:T(8,128)}, f32[4,64,512]{2,1,0:T(8,128)}, u32[]{:S(2)}, u32[]{:S(2)}) %collective-permute-start.3) | collective-permute-done | bytes 524320 | tf_op jit(solution)/shard_map/ppermute | solution.py:19
  125.3 4.9 %fusion.56 = f32[16,64,512]{2,1,0:T(8,128)S(1)} fusion(f32[16,64,512]{2,1,0:T(8,128)S(1)} %copy-done.3, f32[16,64,512]{2,1,0:T(8,128)S(1)} %reshape.603, f32[20,64,512]{2,1,0:T(8,128)S(1)} %get-tuple-element.57, f32[20,64,512]{2,1,0:T(8,128)S(1)} %constant_dynamic-update-slice_fusion, f32[1,16,64,512]{3,2,1,0:T(8,128)S(1)} %copy-done.6), kind=kLoop, calls=%fused_computation.140 | loop fusion | flops 21495808 | bytes 25165824 | tf_op jit(solution)/shard_map/add | solution.py:88
  132.0 4.8 %scatter_fusion.1 = f32[524288]{0:T(1024)} fusion(f32[524288]{0:T(1024)} %bitcast.175, s32[256]{0:T(256)S(1)} %bitcast.192, f32[256]{0:T(256)S(1)} %get-tuple-element.71), kind=kCustom, calls=%fused_computation.5 | custom fusion | flops 256 | bytes 4096 | tf_op jit(solution)/shard_map/scatter-add | solution.py:89
  147.1 4.1 %collective-permute-start.4 = (f32[4,64,512]{2,1,0:T(8,128)}, f32[4,64,512]{2,1,0:T(8,128)}, u32[]{:S(2)}, u32[]{:S(2)}) collective-permute-start(f32[4,64,512]{2,1,0:T(8,128)} %slice.545), channel_id=1, source_target_pairs={{1,0},{2,1},{3,2},{4,3},{5,4},{6,5},{7,6},{9,8},{10,9},{11,10},{12... | collective-permute-start | bytes 1572872 | tf_op jit(solution)/shard_map/ppermute | solution.py:22
  155.2 11.4 %collective-permute-done.5 = f32[4,64,512]{2,1,0:T(8,128)} collective-permute-done((f32[4,64,512]{2,1,0:T(8,128)}, f32[4,64,512]{2,1,0:T(8,128)}, u32[]{:S(2)}, u32[]{:S(2)}) %collective-permute-start.5) | collective-permute-done | bytes 524320 | tf_op jit(solution)/shard_map/ppermute | solution.py:19
  171.1 5.0 %fusion.85 = f32[16,64,512]{2,1,0:T(8,128)S(1)} fusion(f32[16,64,512]{2,1,0:T(8,128)S(1)} %copy-done.4, f32[16,64,512]{2,1,0:T(8,128)S(1)} %copy-done, f32[20,64,512]{2,1,0:T(8,128)S(1)} %get-tuple-element.53, f32[20,64,512]{2,1,0:T(8,128)S(1)} %constant_dynamic-update-slice_fusion.4, f32[16,64,512]{2,1,0:T(8,128)S(1)} %reshape.603), kind=kLoop, calls=%fused_computation.169 | loop fusion | flops 21495808 | bytes 25165824 | tf_op jit(solution)/shard_map/add | solution.py:88
  178.0 4.8 %scatter_fusion.2 = f32[524288]{0:T(1024)} fusion(f32[524288]{0:T(1024)} %bitcast.172, s32[256]{0:T(256)S(1)} %bitcast.193, f32[256]{0:T(256)S(1)} %get-tuple-element.73), kind=kCustom, calls=%fused_computation.6 | custom fusion | flops 256 | bytes 4096 | tf_op jit(solution)/shard_map/scatter-add | solution.py:89
  189.5 5.2 %fusion.160 = (f32[4,16,8,8,128]{4,3,2,1,0:T(8,128)}, f32[4,16,8,8,128]{4,3,2,1,0:T(8,128)}) fusion(s32[16,64,1,128]{3,1,0,2:T(8,128)} %get-tuple-element.24, s32[16,64,1,128]{3,1,0,2:T(8,128)} %get-tuple-element.23, s32[16,64,1,128]{3,1,0,2:T(8,128)} %get-tuple-element.22, s32[16,64,1,128]{3,1,0,2:T(8,128)S(1)} %get-tuple-element.21, ...), kind=kLoop, calls=%fused_computation.267 | loop fusion | flops 6291456 | bytes 8421376
  197.5 3.1 collective-permute-done.7
  201.6 9.6 %constant_dynamic-update-slice_fusion.9 = (f32[20,64,512]{2,1,0:T(8,128)}, f32[20,64,512]{2,1,0:T(8,128)S(1)}, f32[16,64,512]{2,1,0:T(8,128)}) fusion(f32[16,64,512]{2,1,0:T(8,128)} %reshape.607, f32[20,64,512]{2,1,0:T(8,128)S(1)} %constant_dynamic-update-slice_fusion.11, s32[512]{0:T(512)S(1)} %subtract_multiply_fusion, ...), kind=kLoop, calls=%fused_computation.332 | loop fusion | flops 13107199 | bytes 27273216
  218.4 45.9 %psum.7 = f32[]{:T(128)} all-reduce(f32[]{:T(128)S(6)} %add.560), channel_id=1, replica_groups=mesh['shot'=4,'space'=8] {'shot','space'}, use_global_device_ids=true, to_apply=%region_15.17 | all-reduce | flops 1 | bytes 8 | tf_op jit(solution)/shard_map/psum | solution.py:102
  268.7 26.3 %fusion.114 = f32[16,64,512]{2,1,0:T(8,128)S(1)} fusion(f32[16,64,512]{2,1,0:T(8,128)} %param.13, f32[16,64,512]{2,1,0:T(8,128)} %reshape.607, f32[20,64,512]{2,1,0:T(8,128)} %copy-done.5, f32[20,64,512]{2,1,0:T(8,128)} %constant_dynamic-update-slice_fusion.8, f32[16,64,512]{2,1,0:T(8,128)S(1)} %copy-done.1), kind=kLoop, calls=%fused_computation.198 | loop fusion | flops 21495808 | bytes 25165824 | tf_op jit(solution)/shard_map/add | solution.py:88
  (121 shorter events, 77.5 us)
Async XLA Ops:
  7.2 292.6 %reduce-scatter.2.cloned.1.call-start = ((), (), s32[]{:S(2)}) async-start(), calls=%async_computation.1 | async-start | bytes 2621440 | tf_op jit(solution)/shard_map/reduce_scatter | solution.py:100
  9.5 50.0 %collective-permute-start = (f32[4,64,512]{2,1,0:T(8,128)}, f32[4,64,512]{2,1,0:T(8,128)}, u32[]{:S(2)}, u32[]{:S(2)}) collective-permute-start(f32[4,64,512]{2,1,0:T(8,128)} %get-tuple-element.58), channel_id=1, source_target_pairs={{1,0},{2,1},{3,2},{4,3},{5,4},{6,5},{7,6},{9,8},{10,9},{11,10},{12... | collective-permute-start | bytes 1572872 | tf_op jit(solution)/shard_map/ppermute | solution.py:22
  11.4 48.1 %collective-permute-start.1 = (f32[4,64,512]{2,1,0:T(8,128)}, f32[4,64,512]{2,1,0:T(8,128)}, u32[]{:S(2)}, u32[]{:S(2)}) collective-permute-start(f32[4,64,512]{2,1,0:T(8,128)} %get-tuple-element.59), channel_id=1, source_target_pairs={{0,1},{1,2},{2,3},{3,4},{4,5},{5,6},{6,7},{8,9},{9,10},{10,11},{11... | collective-permute-start | bytes 1572872 | tf_op jit(solution)/shard_map/ppermute | solution.py:19
  16.2 3.4 %copy-start.11 = (s32[1,6,16,64,128]{4,3,2,1,0:T(8,128)S(1)}, s32[1,6,16,64,128]{4,3,2,1,0:T(8,128)}, u32[]{:S(2)}) copy-start(s32[1,6,16,64,128]{4,3,2,1,0:T(8,128)} %param.14) | copy-start | bytes 9437188
  19.6 3.7 %copy-start.24 = (s32[1,256]{1,0:T(1,128)S(1)}, s32[1,256]{1,0:T(1,128)}, u32[]{:S(2)}) copy-start(s32[1,256]{1,0:T(1,128)} %param.17) | copy-start | bytes 3076
  19.6 3.7 %copy-start.21 = (s32[1,6,16,256]{3,2,1,0:T(8,128)S(1)}, s32[1,6,16,256]{3,2,1,0:T(8,128)}, u32[]{:S(2)}) copy-start(s32[1,6,16,256]{3,2,1,0:T(8,128)} %param.15) | copy-start | bytes 294916
  19.6 3.8 %copy-start.25 = (f32[64]{0:T(128)S(1)}, f32[64]{0:T(128)}, u32[]{:S(2)}) copy-start(f32[64]{0:T(128)} %param.16) | copy-start | bytes 772
  32.3 2.8 copy-start.12
  32.3 2.8 copy-start.13
  32.3 2.8 copy-start.14
  37.8 9.6 %copy-start.10 = (f32[16,64,4,128]{3,1,0,2:T(8,128)}, f32[16,64,4,128]{3,1,0,2:T(8,128)S(1)}, u32[]{:S(2)}) copy-start(f32[16,64,4,128]{3,1,0,2:T(8,128)S(1)} %get-tuple-element.83) | copy-start | bytes 6291460
  50.8 8.0 %copy-start.23 = (f32[1,4,256]{2,1,0:T(4,128)S(1)}, f32[1,4,256]{2,1,0:T(4,128)}, u32[]{:S(2)}) copy-start(f32[1,4,256]{2,1,0:T(4,128)} %param.18) | copy-start | bytes 12292
  50.9 8.6 %copy-start.2 = (f32[16,64,512]{2,1,0:T(8,128)S(1)}, f32[16,64,512]{2,1,0:T(8,128)}, u32[]{:S(2)}) copy-start(f32[16,64,512]{2,1,0:T(8,128)} %param.13) | copy-start | bytes 6291460
  92.2 7.5 %copy-start.7 = (f32[524288]{0:T(1024)}, f32[524288]{0:T(1024)S(1)}, u32[]{:S(2)}) copy-start(f32[524288]{0:T(1024)S(1)} %scatter_fusion) | copy-start | bytes 6291460
  95.3 26.5 %collective-permute-start.3 = (f32[4,64,512]{2,1,0:T(8,128)}, f32[4,64,512]{2,1,0:T(8,128)}, u32[]{:S(2)}, u32[]{:S(2)}) collective-permute-start(f32[4,64,512]{2,1,0:T(8,128)} %slice.517), channel_id=1, source_target_pairs={{0,1},{1,2},{2,3},{3,4},{4,5},{5,6},{6,7},{8,9},{9,10},{10,11},{11... | collective-permute-start | bytes 1572872 | tf_op jit(solution)/shard_map/ppermute | solution.py:19
  99.8 23.7 %collective-permute-start.2 = (f32[4,64,512]{2,1,0:T(8,128)}, f32[4,64,512]{2,1,0:T(8,128)}, u32[]{:S(2)}, u32[]{:S(2)}) collective-permute-start(f32[4,64,512]{2,1,0:T(8,128)} %slice.514), channel_id=1, source_target_pairs={{1,0},{2,1},{3,2},{4,3},{5,4},{6,5},{7,6},{9,8},{10,9},{11,10},{12... | collective-permute-start | bytes 1572872 | tf_op jit(solution)/shard_map/ppermute | solution.py:22
  136.8 7.0 %copy-start.22 = (s32[1,3]{1,0:T(1,128)S(1)}, s32[1,3]{1,0:T(1,128)}, u32[]{:S(2)}) copy-start(s32[1,3]{1,0:T(1,128)} %param.19) | copy-start | bytes 40
  141.0 25.7 %collective-permute-start.5 = (f32[4,64,512]{2,1,0:T(8,128)}, f32[4,64,512]{2,1,0:T(8,128)}, u32[]{:S(2)}, u32[]{:S(2)}) collective-permute-start(f32[4,64,512]{2,1,0:T(8,128)} %slice.548), channel_id=1, source_target_pairs={{0,1},{1,2},{2,3},{3,4},{4,5},{5,6},{6,7},{8,9},{9,10},{10,11},{11... | collective-permute-start | bytes 1572872 | tf_op jit(solution)/shard_map/ppermute | solution.py:19
  147.1 23.0 %collective-permute-start.4 = (f32[4,64,512]{2,1,0:T(8,128)}, f32[4,64,512]{2,1,0:T(8,128)}, u32[]{:S(2)}, u32[]{:S(2)}) collective-permute-start(f32[4,64,512]{2,1,0:T(8,128)} %slice.545), channel_id=1, source_target_pairs={{1,0},{2,1},{3,2},{4,3},{5,4},{6,5},{7,6},{9,8},{10,9},{11,10},{12... | collective-permute-start | bytes 1572872 | tf_op jit(solution)/shard_map/ppermute | solution.py:22
  167.7 3.4 %copy-start = (f32[16,64,512]{2,1,0:T(8,128)S(1)}, f32[16,64,512]{2,1,0:T(8,128)}, u32[]{:S(2)}) copy-start(f32[16,64,512]{2,1,0:T(8,128)} %reshape.605) | copy-start | bytes 6291460
  167.7 3.4 %copy-start.4 = (f32[16,64,512]{2,1,0:T(8,128)S(1)}, f32[16,64,512]{2,1,0:T(8,128)}, u32[]{:S(2)}) copy-start(f32[16,64,512]{2,1,0:T(8,128)} %param.13) | copy-start | bytes 6291460
  186.9 13.6 %collective-permute-start.7 = (f32[4,64,512]{2,1,0:T(8,128)}, f32[4,64,512]{2,1,0:T(8,128)}, u32[]{:S(2)}, u32[]{:S(2)}) collective-permute-start(f32[4,64,512]{2,1,0:T(8,128)} %slice.582), channel_id=1, source_target_pairs={{0,1},{1,2},{2,3},{3,4},{4,5},{5,6},{6,7},{8,9},{9,10},{10,11},{11... | collective-permute-start | bytes 1572872 | tf_op jit(solution)/shard_map/ppermute | solution.py:19
  213.8 54.0 %collective-permute-start.6 = (f32[4,64,512]{2,1,0:T(8,128)S(1)}, f32[4,64,512]{2,1,0:T(8,128)S(1)}, u32[]{:S(2)}, u32[]{:S(2)}) collective-permute-start(f32[4,64,512]{2,1,0:T(8,128)S(1)} %slice.579), channel_id=1, source_target_pairs={{1,0},{2,1},{3,2},{4,3},{5,4},{6,5},{7,6},{9,8},{10,9},{11,10},{12... | collective-permute-start | bytes 1572872 | tf_op jit(solution)/shard_map/ppermute | solution.py:22
  264.9 3.7 %copy-start.1 = (f32[16,64,512]{2,1,0:T(8,128)S(1)}, f32[16,64,512]{2,1,0:T(8,128)}, u32[]{:S(2)}) copy-start(f32[16,64,512]{2,1,0:T(8,128)} %reshape.605) | copy-start | bytes 6291460
  (11 other events, 26.3 us)
Sparse Core Ops, SparseCore 0:
  212.8 32.5 reduce-scatter.1
where the time goes:
time: 310 us; the launch traced here: 308 us
  other arithmetic  113 us (36%)
  local copies, waits for them, and re-layouts  74.6 us (24%)
  blocking collectives  45.9 us (15%)
  waiting for transfers between devices  30.7 us (10%)
  starting transfers between devices  24.6 us (8%)
  between operations  18.8 us (6%)
    add x4, other arithmetic, body(): stepped = 2.0 * now - later + courant * laplace(now)  65.4 us
    psum x1, blocking collectives, body(): misfit = 0.5 * lax.psum(misfit_part, ('shot', 'space')) / count  45.9 us
    ppermute x4, waiting for transfers between devices, with_halo(): lax.ppermute(lax.slice_in_dim(block, block.shape[dim] - width, None, axis...  30.7 us
    scatter-add x4, other arithmetic, body(): stepped.reshape(-1).at[cells].add(residual).reshape(depth, rows, cols)  15.3 us
    unnamed x2, other arithmetic  14.8 us
    unnamed x61, local copies, waits for them, and re-layouts  13.9 us
    gather x4, local copies, waits for them, and re-layouts, body(): synthetic = jnp.take(fields[level].reshape(-1), cells)  13.8 us
    mul x10, local copies, waits for them, and re-layouts, decode(): centred.reshape(depth, rows, cols // QBLOCK, QBLOCK)  13.2 us
  transfers between devices with their start and end apart: 9, of which 3 were waited for; matrix products, arithmetic and copies ran while one was open for 33% of the time, Pallas kernels for 0%

commit v1 on v0

v1 whole, which is shorter than its diff:
```python
import functools

import jax
import jax.numpy as jnp
from jax import lax
from jax.experimental import pallas as pl
from jax.experimental.pallas import tpu as pltpu
from jax.sharding import PartitionSpec as P

ITERS = 4
QBLOCK = 128
MUTE = 8
W = 4
NC = 2
F32 = jnp.float32
BF16 = jnp.bfloat16
MESH = pl.DeviceIdType.MESH

COEFFS = (-205.0 / 72.0, 8.0 / 5.0, -1.0 / 5.0, 8.0 / 315.0, -1.0 / 560.0)


def split(value):
    high = value.astype(BF16)
    return high, (value - high.astype(F32)).astype(BF16)


def dot(a, b):
    return jnp.dot(a, b, preferred_element_type=F32)


def band(rows, cols, first):
    i = first + lax.broadcasted_iota(jnp.int32, (rows, cols), 0)
    j = lax.broadcasted_iota(jnp.int32, (rows, cols), 1)
    d = jnp.abs(i - j)
    value = jnp.zeros((rows, cols), F32)
    for k in range(1, 5):
        value = jnp.where(d == k, COEFFS[k], value)
    return split(value)


def kernel(
    nshot,
    nspace,
    cells_s,
    source_s,
    table,
    now_h,
    later_h,
    cour,
    words,
    index,
    cells_row,
    cells_col,
    observed,
    grad,
    first_h,
    second_h,
    misfit,
    E,
    D,
    scales,
    IM,
    RA,
    S,
    RB,
    PR,
    QH,
    QL,
    CH,
    CL,
    GW,
    GS,
    MB,
    SB,
    MT,
    ST,
    halo_send,
    halo_recv,
    a_send,
    a_recv,
    b_send,
    b_recv,
    m_send,
    m_recv,
    s_send,
    s_recv,
    local_sem,
):
    depth, rows, cols = cour.shape
    nrec = cells_col.shape[0]
    ych = rows // NC
    shot = lax.axis_index("shot")
    space = lax.axis_index("space")
    has_low = space > 0
    has_high = space < nspace - 1

    barrier = pltpu.get_barrier_semaphore()
    for d in range(1, nshot):
        pl.semaphore_signal(
            barrier, inc=1, device_id={"shot": lax.rem(shot + d, nshot)}, device_id_type=MESH
        )

    @pl.loop(1, nspace)
    def _(d):
        pl.semaphore_signal(
            barrier, inc=1, device_id={"space": lax.rem(space + d, nspace)}, device_id_type=MESH
        )

    pl.semaphore_wait(barrier, nshot + nspace - 2)

    def halo(t, c, up):
        ys = pl.ds(c * ych, ych)
        src_z = W + depth - W if up else W
        dst_z = 0 if up else W + depth
        return pltpu.make_async_remote_copy(
            src_ref=E.at[t + 1, pl.ds(src_z, W), ys, :],
            dst_ref=E.at[t + 1, pl.ds(dst_z, W), ys, :],
            send_sem=halo_send.at[int(up), t, c],
            recv_sem=halo_recv.at[int(up), t, c],
            device_id={"space": space + (1 if up else -1)},
            device_id_type=MESH,
        )

    def halo_first(c, up):
        ys = pl.ds(c * ych, ych)
        src_z = depth - W if up else 0
        dst_z = 0 if up else W + depth
        return pltpu.make_async_remote_copy(
            src_ref=now_h.at[pl.ds(src_z, W), ys, :],
            dst_ref=E.at[1, pl.ds(dst_z, W), ys, :],
            send_sem=halo_send.at[int(up), 0, c],
            recv_sem=halo_recv.at[int(up), 0, c],
            device_id={"space": space + (1 if up else -1)},
            device_id_type=MESH,
        )

    for c in range(NC):

        @pl.when(has_high)
        def _():
            halo_first(c, True).start()

        @pl.when(has_low)
        def _():
            halo_first(c, False).start()

    in_now = pltpu.make_async_copy(now_h, E.at[1, pl.ds(W, depth)], local_sem.at[0])
    in_later = pltpu.make_async_copy(later_h, E.at[0, pl.ds(W, depth)], local_sem.at[1])
    in_now.start()
    in_later.start()

    @pl.loop(0, cols // 64)
    def _(i):
        start = pl.multiple_of(i * 64, 64)
        high, low = band(64, cols, start)
        CH[pl.ds(start, 64), :] = high
        CL[pl.ds(start, 64), :] = low

    yh, yl = band(rows, rows, 0)

    @pl.loop(0, depth)
    def _(z):
        entry = index[z]
        scale = jnp.zeros(entry.shape, F32)
        for e in range(table.shape[0]):
            scale = jnp.where(entry == e, table[e], scale)
        scales[z] = scale

    slab = depth * rows * cols

    @pl.loop(0, nrec)
    def _(r):
        cell = lax.rem(cells_s[r], slab)
        row = cell // cols
        z = row // rows
        y = lax.rem(row, rows)
        for k in range(1, ITERS + 1):
            GW[k - 1, pl.ds(r, 1), :] = words[k, z, pl.ds(y, 1), :]
        GS[pl.ds(r, 1), :] = scales[z, pl.ds(y, 1), :]

    xcol = lax.rem(cells_col[...], cols)
    mcol = xcol // QBLOCK
    jcol = lax.rem(xcol, QBLOCK)
    lane = lax.broadcasted_iota(jnp.int32, (nrec, QBLOCK), 1)
    xl = lax.broadcasted_iota(jnp.int32, (nrec, cols), 1)
    squares = jnp.zeros((1, 1), F32)
    for k in range(1, ITERS + 1):
        code = jnp.bitwise_and(jnp.right_shift(GW[k - 1], 8 * mcol), 255) - 128
        code = jnp.sum(jnp.where(lane == jcol, code.astype(F32), 0.0), axis=1, keepdims=True)
        scale = jnp.sum(
            jnp.where(lane == k * 4 + mcol, GS[...], 0.0), axis=1, keepdims=True
        )
        residual = code * scale - observed[:, k - 1 : k]
        squares = squares + jnp.sum(residual * residual, axis=0, keepdims=True)
        high, low = split(jnp.where(xl == xcol, residual, 0.0))
        QH[ITERS - k] = high
        QL[ITERS - k] = low
    crow = lax.rem(cells_row[...], slab) // cols
    for z in range(depth):
        i = z * rows + lax.broadcasted_iota(jnp.int32, (rows, nrec), 0)
        PR[z] = jnp.where(i == crow, 1.0, 0.0).astype(BF16)

    tile = jnp.broadcast_to(squares, (8, 128))
    MT[...] = tile
    MB[pl.ds(shot, 1)] = tile.reshape(1, 8, 128)

    def misfit_copy(d):
        return pltpu.make_async_remote_copy(
            src_ref=MT,
            dst_ref=MB.at[shot],
            send_sem=m_send.at[d - 1],
            recv_sem=m_recv.at[d - 1],
            device_id={"shot": lax.rem(shot + d, nshot)},
            device_id_type=MESH,
        )

    def total_copy(d):
        return pltpu.make_async_remote_copy(
            src_ref=ST,
            dst_ref=SB.at[space],
            send_sem=s_send.at[d - 1],
            recv_sem=s_recv.at[d - 1],
            device_id={"space": lax.rem(space + d, nspace)},
            device_id_type=MESH,
        )

    for d in range(1, nshot):
        misfit_copy(d).start()

    in_now.wait()
    in_later.wait()

    def local(t):
        for g in (0, depth // W - 1) + tuple(range(1, depth // W - 1)):
            z0 = g * W
            u = E[t + 1, W + z0 : W + z0 + W].reshape(W * rows, cols)
            uh, ul = split(u)
            lap = dot(uh, CH[...]) + dot(ul, CH[...]) + dot(uh, CL[...])
            for j in range(W):
                z = z0 + j
                part = slice(j * rows, (j + 1) * rows)
                up = u[part]
                acc = lap[part] + (3.0 * COEFFS[0]) * up
                acc = acc + dot(yh, uh[part]) + dot(yh, ul[part]) + dot(yl, uh[part])
                for i in range(1, 5):
                    if z + i < depth:
                        acc = acc + COEFFS[i] * E[t + 1, W + z + i]
                    if z - i >= 0:
                        acc = acc + COEFFS[i] * E[t + 1, W + z - i]
                inject = dot(PR[z], QH[t]) + dot(PR[z], QL[t])
                E[t + 2, W + z] = 2.0 * up - E[t, W + z] + cour[z] * acc + inject

    local(0)

    @pl.loop(0, depth)
    def _(z):
        for m in range(cols // QBLOCK):
            xs = slice(m * QBLOCK, (m + 1) * QBLOCK)
            f = []
            for k in range(ITERS + 2):
                code = jnp.bitwise_and(jnp.right_shift(words[k, z], 8 * m), 255) - 128
                f.append(code.astype(F32) * scales[z, :, k * 4 + m : k * 4 + m + 1])
            for t in range(ITERS):
                k = ITERS - t
                diff = f[k + 1] - 2.0 * f[k] + f[k - 1]
                if t == 0:
                    IM[z, :, xs] = E[1, W + z, :, xs] * diff
                else:
                    D[t - 1, z, :, xs] = diff

    for d in range(1, nshot):
        misfit_copy(d).wait()
    total = MB[0]
    for d in range(1, nshot):
        total = total + MB[d]
    ST[...] = total
    SB[pl.ds(space, 1)] = total.reshape(1, 8, 128)

    @pl.loop(1, nspace)
    def _(d):
        total_copy(d).start()

    def fix(t, c):
        ys = pl.ds(c * ych, ych)

        @pl.when(has_low)
        def _():
            halo(t, c, True).wait_recv()
            for j in range(W):
                acc = COEFFS[j + 1] * E[t + 1, W - 1, ys, :]
                for i in range(j + 2, 5):
                    acc = acc + COEFFS[i] * E[t + 1, W + j - i, ys, :]
                E[t + 2, W + j, ys, :] += cour[j, ys, :] * acc

        @pl.when(has_high)
        def _():
            halo(t, c, False).wait_recv()
            for j in range(W):
                z = depth - 1 - j
                acc = COEFFS[j + 1] * E[t + 1, W + depth, ys, :]
                for i in range(j + 2, 5):
                    acc = acc + COEFFS[i] * E[t + 1, W + z + i, ys, :]
                E[t + 2, W + z, ys, :] += cour[z, ys, :] * acc

    @pl.loop(0, ITERS - 1)
    def _(t):
        for c in range(NC):
            fix(t, c)

            @pl.when(has_high)
            def _():
                halo(t + 1, c, True).start()

            @pl.when(has_low)
            def _():
                halo(t + 1, c, False).start()

        local(t + 1)

        @pl.loop(0, depth)
        def _(z):
            IM[z] = IM[z] + E[t + 2, W + z] * D[t, z]

    out_second = pltpu.make_async_copy(E.at[ITERS, pl.ds(W, depth)], second_h, local_sem.at[2])
    out_second.start()

    first_z = space * depth

    @pl.loop(0, depth)
    def _(z):
        dz = first_z + z - source_s[0]
        dy = lax.broadcasted_iota(jnp.int32, (rows, cols), 0) - source_s[1]
        dx = lax.broadcasted_iota(jnp.int32, (rows, cols), 1) - source_s[2]
        dist = (dz * dz + dy * dy + dx * dx).astype(F32)
        IM[z] = IM[z] * (1.0 - jnp.exp(dist * (-1.0 / (2.0 * MUTE * MUTE))))

    core = lax.rem(shot, 2)
    pair = shot // 2
    pairs = nshot // 2
    yq = rows // nshot

    def quarter(index):
        return pl.ds(pl.multiple_of(index * yq, yq), yq)

    def copy_a(h):
        return pltpu.make_async_remote_copy(
            src_ref=IM.at[:, quarter(2 * h + 1 - core), :],
            dst_ref=RA.at[h],
            send_sem=a_send.at[h],
            recv_sem=a_recv.at[h],
            device_id={"shot": shot + 1 - 2 * core},
            device_id_type=MESH,
        )

    def copy_b(d):
        target = lax.rem(pair + d, pairs)
        return pltpu.make_async_remote_copy(
            src_ref=S.at[target],
            dst_ref=RB.at[d - 1],
            send_sem=b_send.at[d - 1],
            recv_sem=b_recv.at[d - 1],
            device_id={"shot": 2 * target + core},
            device_id_type=MESH,
        )

    for h in range(pairs):
        copy_a(h).start()
    for h in range(pairs):
        copy_a(h).wait()
        S[h] = IM[:, quarter(2 * h + core), :] + RA[h]
    for d in range(1, pairs):
        copy_b(d).start()

    for c in range(NC):
        fix(ITERS - 1, c)
    out_first = pltpu.make_async_copy(E.at[ITERS + 1, pl.ds(W, depth)], first_h, local_sem.at[3])
    out_first.start()

    total = S[pair]
    for d in range(1, pairs):
        copy_b(d).wait()
        total = total + RB[d - 1]
    grad[...] = total

    @pl.loop(1, nspace)
    def _(d):
        total_copy(d).wait()

    whole = SB[0]
    for d in range(1, nspace):
        whole = whole + SB[d]
    misfit[...] = whole

    for c in range(NC):

        @pl.when(has_high)
        def _():
            halo_first(c, True).wait_send()

        @pl.when(has_low)
        def _():
            halo_first(c, False).wait_send()

        @pl.loop(1, ITERS)
        def _(t):
            @pl.when(has_high)
            def _():
                halo(t, c, True).wait_send()

            @pl.when(has_low)
            def _():
                halo(t, c, False).wait_send()

    out_second.wait()
    out_first.wait()


def body(
    nshot,
    nspace,
    adjoint_now,
    adjoint_later,
    courant,
    checkpoint_codes,
    scale_index,
    scale_table,
    receiver_cell,
    observed,
    source_cell,
):
    depth, rows, cols = courant.shape
    levels = checkpoint_codes.shape[1]
    nrec = receiver_cell.shape[1]
    blocks = cols // QBLOCK
    index = scale_index[0].reshape(levels, depth, rows, blocks).transpose(1, 2, 0, 3)
    index = index.reshape(depth, rows, levels * blocks)
    index = jnp.pad(index, ((0, 0), (0, 0), (0, 128 - levels * blocks)))
    pairs = nshot // 2
    yq = rows // nshot
    vmem = pl.BlockSpec(memory_space=pltpu.VMEM)
    smem = pl.BlockSpec(memory_space=pltpu.SMEM)
    anyspace = pl.BlockSpec(memory_space=pl.ANY)
    dma = pltpu.SemaphoreType.DMA
    field = jax.ShapeDtypeStruct((depth, rows, cols), F32)
    gradient, first, second, misfit = pl.pallas_call(
        functools.partial(kernel, nshot, nspace),
        out_shape=(
            jax.ShapeDtypeStruct((depth, yq, cols), F32),
            field,
            field,
            jax.ShapeDtypeStruct((8, 128), F32),
        ),
        in_specs=[smem, smem, smem, anyspace, anyspace] + [vmem] * 6,
        out_specs=(vmem, anyspace, anyspace, vmem),
        scratch_shapes=[
            pltpu.VMEM((ITERS + 2, depth + 2 * W, rows, cols), F32),
            pltpu.VMEM((ITERS - 1, depth, rows, cols), F32),
            pltpu.VMEM((depth, rows, 128), F32),
            pltpu.VMEM((depth, rows, cols), F32),
            pltpu.VMEM((pairs, depth, yq, cols), F32),
            pltpu.VMEM((pairs, depth, yq, cols), F32),
            pltpu.VMEM((max(pairs - 1, 1), depth, yq, cols), F32),
            pltpu.VMEM((depth, rows, nrec), BF16),
            pltpu.VMEM((ITERS, nrec, cols), BF16),
            pltpu.VMEM((ITERS, nrec, cols), BF16),
            pltpu.VMEM((cols, cols), BF16),
            pltpu.VMEM((cols, cols), BF16),
            pltpu.VMEM((ITERS, nrec, QBLOCK), jnp.int32),
            pltpu.VMEM((nrec, 128), F32),
            pltpu.VMEM((nshot, 8, 128), F32),
            pltpu.VMEM((nspace, 8, 128), F32),
            pltpu.VMEM((8, 128), F32),
            pltpu.VMEM((8, 128), F32),
            dma((2, ITERS, NC)),
            dma((2, ITERS, NC)),
            dma((pairs,)),
            dma((pairs,)),
            dma((max(pairs - 1, 1),)),
            dma((max(pairs - 1, 1),)),
            dma((nshot - 1,)),
            dma((nshot - 1,)),
            dma((nspace - 1,)),
            dma((nspace - 1,)),
            dma((4,)),
        ],
        compiler_params=pltpu.CompilerParams(
            collective_id=0, has_side_effects=True, vmem_limit_bytes=66000000
        ),
    )(
        receiver_cell[0],
        source_cell[0],
        scale_table,
        adjoint_now[0],
        adjoint_later[0],
        courant,
        checkpoint_codes[0],
        index,
        receiver_cell,
        receiver_cell.reshape(nrec, 1),
        observed[0].T,
    )
    count = nshot * ITERS * nrec * nspace
    return (gradient, first[None], second[None], 0.5 * misfit[0, 0] / count)


def solution(mesh):
    placed = (
        P("shot", "space", None, None),
        P("shot", "space", None, None),
        P("space", None, None),
        P("shot", None, "space", None, None),
        P("shot", None, "space", None),
        P(),
        P("shot", "space"),
        P("shot", None, "space"),
        P("shot", None),
    )
    return jax.shard_map(
        functools.partial(body, mesh.shape["shot"], mesh.shape["space"]),
        mesh=mesh,
        in_specs=placed,
        out_specs=(
            P("space", "shot", None),
            P("shot", "space", None, None),
            P("shot", "space", None, None),
            P(),
        ),
        check_vma=False,
    )
```

time: 310 us -> 128 us (0.41)
  other arithmetic: 113 us -> 0 us
  Pallas kernels: 0 us -> 112 us
  local copies, waits for them, and re-layouts: 74.6 us -> 13.1 us
  blocking collectives: 45.9 us -> 0 us
  waiting for transfers between devices: 30.7 us -> 0 us
  starting transfers between devices: 24.6 us -> 0 us
  between operations: 18.8 us -> 2.44 us
    pallas_call x0 -> x1, Pallas kernels: none -> 112 us  [body(): pl.pallas_call(functools.partial(kernel, nshot, nspace), out_shape=(jax.S...]
    add x5 -> x0, other arithmetic: 65.5 us -> none  [the longest x4 65.4 us: body(): stepped = 2.0 * now - later + courant * laplace(now)]
    psum x1 -> x0, blocking collectives: 45.9 us -> none  [body(): misfit = 0.5 * lax.psum(misfit_part, ('shot', 'space')) / count]
    ppermute x8 -> x0, waiting for transfers between devices: 30.7 us -> none  [the longest x4 30.7 us: with_halo(): lax.ppermute(lax.slice_in_dim(block, block.shape[dim] - width, None, axis...]
    ppermute x8 -> x0, starting transfers between devices: 24.6 us -> none  [the longest x4 12.3 us: with_halo(): lax.ppermute(lax.slice_in_dim(block, block.shape[dim] - width, None, axis...]
    slice x12 -> x1, local copies, waits for them, and re-layouts: 18.2 us -> 1.18 us  [body(): return (gradient, first[None], second[None], 0.5 * misfit[0, 0] / count)]
    scatter-add x4 -> x0, other arithmetic: 15.3 us -> none  [body(): stepped.reshape(-1).at[cells].add(residual).reshape(depth, rows, cols)]
    unnamed x2 -> x0, other arithmetic: 14.8 us -> none
  transfers between devices with their start and end apart: 9 -> 0, of which waited for: 3 -> 0; matrix products, arithmetic and copies ran while one was open for 33% -> 0% of each run, Pallas kernels for 0% -> 0%
where the time goes in v1:
time: 128 us; the launch traced here: 127 us
  Pallas kernels  112 us (88%)
  local copies, waits for them, and re-layouts  13.1 us (10%)
  between operations  2.44 us (2%)
    pallas_call x1, Pallas kernels, body(): pl.pallas_call(functools.partial(kernel, nshot, nspace), out_shape=(jax.S...  112 us
    unnamed x7, local copies, waits for them, and re-layouts  9.13 us

profile of v1, /device:TPU:2, one launch (start us, length us, event | category | flops | bytes accessed | tf_op | source)
XLA Modules:
  0.0 127.3 jit_solution(15043721777107750267)
XLA Ops:
  0.6 1.5 %copy.18 = f32[1,4,256]{1,2,0:T(8,128)} copy(f32[1,4,256]{2,1,0:T(4,128)} %param.16) | data formatting | bytes 8192 | tf_op args[7]
  2.1 1.5 %copy.19.cells_col = s32[256,1]{1,0:T(8,128)} copy(s32[256,1]{0,1:T(1,128)} %bitcast.24) | data formatting | bytes 2048 | tf_op jit(solution)/shard_map/reshape | solution.py:499
  3.6 1.2 copy.15
  4.7 0.2 copy.16
  5.0 0.2 copy.17
  5.2 0.8 pad.4.index
  6.1 111.8 %shard_map.120 = (f32[16,16,512]{2,1,0:T(8,128)}, f32[16,64,512]{2,1,0:T(8,128)}, f32[16,64,512]{2,1,0:T(8,128)}, f32[8,128]{1,0:T(8,128)}) custom-call(s32[256]{0:T(256)} %bitcast.25, s32[3]{0:T(128)} %bitcast.26, f32[64]{0:T(128)} %table.1, f32[16,64,512]{2,1,0:T(8,128)} %bitcast.20, f32[16,64,512]{2,1,0:T(8,128)} %bitcast.21, f32[16,64,512]{2,1,0:T(8,128)} %cour.1, ...), custom_call_target="tpu_custom_call" | custom-call | tf_op jit(solution)/shard_map/pallas_call | solution.py:445
  117.9 1.2 slice.3
  119.7 1.9 %copy.23 = f32[16,16,512]{2,1,0:T(8,128)} copy(f32[16,16,512]{2,1,0:T(8,128)} %get-tuple-element.16) | data formatting | bytes 1048576
  121.6 0.0 copy-start
  121.6 3.3 %copy.24 = f32[1,16,64,512]{3,2,1,0:T(8,128)} copy(f32[1,16,64,512]{3,2,1,0:T(8,128)} %bitcast.19) | data formatting | bytes 4194304
  124.9 0.0 copy-done
  124.9 1.3 %copy.25 = f32[1,16,64,512]{3,2,1,0:T(8,128)} copy(f32[1,16,64,512]{3,2,1,0:T(8,128)S(1)} %bitcast.18) | data formatting | bytes 4194304
Async XLA Ops:
  121.6 3.3 %copy-start = (f32[16,64,512]{2,1,0:T(8,128)S(1)}, f32[16,64,512]{2,1,0:T(8,128)}, u32[]{:S(2)}) copy-start(f32[16,64,512]{2,1,0:T(8,128)} %get-tuple-element.10) | copy-start | bytes 6291460

commit v2 on v1

--- a/solution.py
+++ b/solution.py
@@ -44,21 +44,25 @@
     cells_s,
     source_s,
     table,
+    observed,
     now_h,
     later_h,
-    cour,
-    words,
+    cour_h,
+    words_h,
     index,
     cells_row,
-    cells_col,
-    observed,
     grad,
     first_h,
     second_h,
     misfit,
     E,
     D,
-    scales,
+    cour,
+    words,
+    SC,
+    TS,
+    PC,
+    OB,
     IM,
     RA,
     S,
@@ -87,7 +91,8 @@
     local_sem,
 ):
     depth, rows, cols = cour.shape
-    nrec = cells_col.shape[0]
+    nrec = cells_row.shape[1]
+    blocks = cols // QBLOCK
     ych = rows // NC
     shot = lax.axis_index("shot")
     space = lax.axis_index("space")
@@ -105,6 +110,15 @@
         pl.semaphore_signal(
             barrier, inc=1, device_id={"space": lax.rem(space + d, nspace)}, device_id_type=MESH
         )
+
+    in_now = pltpu.make_async_copy(now_h, E.at[1, pl.ds(W, depth)], local_sem.at[0])
+    in_later = pltpu.make_async_copy(later_h, E.at[0, pl.ds(W, depth)], local_sem.at[1])
+    in_cour = pltpu.make_async_copy(cour_h, cour, local_sem.at[2])
+    in_words = pltpu.make_async_copy(words_h, words, local_sem.at[3])
+    in_words.start()
+    in_now.start()
+    in_cour.start()
+    in_later.start()
 
     pl.semaphore_wait(barrier, nshot + nspace - 2)
 
@@ -144,11 +158,6 @@
         def _():
             halo_first(c, False).start()
 
-    in_now = pltpu.make_async_copy(now_h, E.at[1, pl.ds(W, depth)], local_sem.at[0])
-    in_later = pltpu.make_async_copy(later_h, E.at[0, pl.ds(W, depth)], local_sem.at[1])
-    in_now.start()
-    in_later.start()
-
     @pl.loop(0, cols // 64)
     def _(i):
         start = pl.multiple_of(i * 64, 64)
@@ -158,17 +167,18 @@
 
     yh, yl = band(rows, rows, 0)
 
-    @pl.loop(0, depth)
-    def _(z):
-        entry = index[z]
-        scale = jnp.zeros(entry.shape, F32)
-        for e in range(table.shape[0]):
-            scale = jnp.where(entry == e, table[e], scale)
-        scales[z] = scale
+    entry = index[...]
+    scale = jnp.zeros(entry.shape, F32)
+    for e in range(table.shape[0]):
+        scale = jnp.where(entry == e, table[e], scale)
+    levels = entry.shape[0]
+    SC[0:levels] = scale
+    SC[levels:] = jnp.zeros((SC.shape[0] - levels,) + entry.shape[1:], F32)
 
     slab = depth * rows * cols
-
-    @pl.loop(0, nrec)
+    in_words.wait()
+
+    @pl.loop(0, nrec, unroll=4)
     def _(r):
         cell = lax.rem(cells_s[r], slab)
         row = cell // cols
@@ -176,21 +186,24 @@
         y = lax.rem(row, rows)
         for k in range(1, ITERS + 1):
             GW[k - 1, pl.ds(r, 1), :] = words[k, z, pl.ds(y, 1), :]
-        GS[pl.ds(r, 1), :] = scales[z, pl.ds(y, 1), :]
-
-    xcol = lax.rem(cells_col[...], cols)
+            GS[k - 1, pl.ds(r, 1), :] = SC[k, pl.ds(z, 1), :]
+            OB[k - 1, pl.ds(r, 1), :] = jnp.full((1, 128), observed[k - 1, r], F32)
+        PC[pl.ds(r, 1), :] = jnp.full((1, 128), cell - z * (rows * cols), jnp.int32)
+
+    place = PC[:, 0:1]
+    xcol = lax.rem(place, cols)
     mcol = xcol // QBLOCK
     jcol = lax.rem(xcol, QBLOCK)
+    scol = place // cols * blocks + mcol
     lane = lax.broadcasted_iota(jnp.int32, (nrec, QBLOCK), 1)
+    sl = lax.broadcasted_iota(jnp.int32, (nrec, rows * blocks), 1)
     xl = lax.broadcasted_iota(jnp.int32, (nrec, cols), 1)
     squares = jnp.zeros((1, 1), F32)
     for k in range(1, ITERS + 1):
         code = jnp.bitwise_and(jnp.right_shift(GW[k - 1], 8 * mcol), 255) - 128
         code = jnp.sum(jnp.where(lane == jcol, code.astype(F32), 0.0), axis=1, keepdims=True)
-        scale = jnp.sum(
-            jnp.where(lane == k * 4 + mcol, GS[...], 0.0), axis=1, keepdims=True
-        )
-        residual = code * scale - observed[:, k - 1 : k]
+        scale = jnp.sum(jnp.where(sl == scol, GS[k - 1], 0.0), axis=1, keepdims=True)
+        residual = code * scale - OB[k - 1, :, 0:1]
         squares = squares + jnp.sum(residual * residual, axis=0, keepdims=True)
         high, low = split(jnp.where(xl == xcol, residual, 0.0))
         QH[ITERS - k] = high
@@ -229,6 +242,7 @@
 
     in_now.wait()
     in_later.wait()
+    in_cour.wait()
 
     def local(t):
         for g in (0, depth // W - 1) + tuple(range(1, depth // W - 1)):
@@ -252,21 +266,38 @@
 
     local(0)
 
-    @pl.loop(0, depth)
-    def _(z):
-        for m in range(cols // QBLOCK):
-            xs = slice(m * QBLOCK, (m + 1) * QBLOCK)
-            f = []
-            for k in range(ITERS + 2):
-                code = jnp.bitwise_and(jnp.right_shift(words[k, z], 8 * m), 255) - 128
-                f.append(code.astype(F32) * scales[z, :, k * 4 + m : k * 4 + m + 1])
-            for t in range(ITERS):
-                k = ITERS - t
-                diff = f[k + 1] - 2.0 * f[k] + f[k - 1]
-                if t == 0:
-                    IM[z, :, xs] = E[1, W + z, :, xs] * diff
-                else:
-                    D[t - 1, z, :, xs] = diff
+    def decode():
+        i = lax.broadcasted_iota(jnp.int32, (rows, rows * blocks), 0)
+        j = lax.broadcasted_iota(jnp.int32, (rows, rows * blocks), 1)
+        flat = SC[...].reshape(128, rows * blocks)
+        high = flat.astype(BF16)
+        rest = flat - high.astype(F32)
+        pieces = (high,) + split(rest)
+        for m in range(blocks):
+            pick = jnp.where(j == blocks * i + m, 1.0, 0.0).astype(BF16)
+            moved = jnp.zeros((rows, 128), F32)
+            for piece in pieces:
+                moved = moved + lax.dot_general(
+                    pick, piece, (((1,), (1,)), ((), ())), preferred_element_type=F32
+                )
+            TS[m] = moved
+
+        @pl.loop(0, depth)
+        def _(z):
+            for m in range(blocks):
+                xs = slice(m * QBLOCK, (m + 1) * QBLOCK)
+                scale = pltpu.roll(TS[m], lax.rem(128 - z, 128), 1)
+                f = []
+                for k in range(ITERS + 2):
+                    code = jnp.bitwise_and(jnp.right_shift(words[k, z], 8 * m), 255) - 128
+                    f.append(code.astype(F32) * scale[:, k * depth : k * depth + 1])
+                for t in range(ITERS):
+                    k = ITERS - t
+                    diff = f[k + 1] - 2.0 * f[k] + f[k - 1]
+                    if t == 0:
+                        IM[z, :, xs] = E[1, W + z, :, xs] * diff
+                    else:
+                        D[t - 1, z, :, xs] = diff
 
     for d in range(1, nshot):
         misfit_copy(d).wait()
@@ -315,14 +346,25 @@
             def _():
                 halo(t + 1, c, False).start()
 
+            if c == 0:
+
+                @pl.when(t == 0)
+                def _():
+                    decode()
+
         local(t + 1)
 
         @pl.loop(0, depth)
         def _(z):
             IM[z] = IM[z] + E[t + 2, W + z] * D[t, z]
 
-    out_second = pltpu.make_async_copy(E.at[ITERS, pl.ds(W, depth)], second_h, local_sem.at[2])
+    out_second = pltpu.make_async_copy(E.at[ITERS, pl.ds(W, depth)], second_h, local_sem.at[4])
     out_second.start()
+    inner = depth - 2 * W
+    out_inner = pltpu.make_async_copy(
+        E.at[ITERS + 1, pl.ds(2 * W, inner)], first_h.at[pl.ds(W, inner)], local_sem.at[5]
+    )
+    out_inner.start()
 
     first_z = space * depth
 
@@ -373,8 +415,14 @@
 
     for c in range(NC):
         fix(ITERS - 1, c)
-    out_first = pltpu.make_async_copy(E.at[ITERS + 1, pl.ds(W, depth)], first_h, local_sem.at[3])
-    out_first.start()
+    out_low = pltpu.make_async_copy(
+        E.at[ITERS + 1, pl.ds(W, W)], first_h.at[pl.ds(0, W)], local_sem.at[6]
+    )
+    out_high = pltpu.make_async_copy(
+        E.at[ITERS + 1, pl.ds(depth, W)], first_h.at[pl.ds(depth - W, W)], local_sem.at[7]
+    )
+    out_low.start()
+    out_high.start()
 
     total = S[pair]
     for d in range(1, pairs):
@@ -412,7 +460,36 @@
                 halo(t, c, False).wait_send()
 
     out_second.wait()
-    out_first.wait()
+    out_inner.wait()
+    out_low.wait()
+    out_high.wait()
+
+
+def finish(factor, grad, first, second, total, grad_o, first_o, second_o, misfit, GB, FB, sem_in, sem_out):
+    parts = FB.shape[0] // 2
+    planes = FB.shape[1]
+    moves = []
+    for n, (source, target) in enumerate(((first, first_o), (second, second_o))):
+        for p in range(parts):
+            at = pl.ds(p * planes, planes)
+            moves.append((source.at[at], FB.at[n * parts + p], target.at[at]))
+    moves.append((grad, GB, grad_o))
+    into = [
+        pltpu.make_async_copy(source, held, sem_in.at[n])
+        for n, (source, held, target) in enumerate(moves)
+    ]
+    out = [
+        pltpu.make_async_copy(held, target, sem_out.at[n])
+        for n, (source, held, target) in enumerate(moves)
+    ]
+    for copy in into:
+        copy.start()
+    misfit[...] = total[0:1, 0:1] * factor
+    for n in range(len(moves)):
+        into[n].wait()
+        out[n].start()
+    for copy in out:
+        copy.wait()
 
 
 def body(
@@ -432,9 +509,6 @@
     levels = checkpoint_codes.shape[1]
     nrec = receiver_cell.shape[1]
     blocks = cols // QBLOCK
-    index = scale_index[0].reshape(levels, depth, rows, blocks).transpose(1, 2, 0, 3)
-    index = index.reshape(depth, rows, levels * blocks)
-    index = jnp.pad(index, ((0, 0), (0, 0), (0, 128 - levels * blocks)))
     pairs = nshot // 2
     yq = rows // nshot
     vmem = pl.BlockSpec(memory_space=pltpu.VMEM)
@@ -442,7 +516,7 @@
     anyspace = pl.BlockSpec(memory_space=pl.ANY)
     dma = pltpu.SemaphoreType.DMA
     field = jax.ShapeDtypeStruct((depth, rows, cols), F32)
-    gradient, first, second, misfit = pl.pallas_call(
+    gradient, first, second, total = pl.pallas_call(
         functools.partial(kernel, nshot, nspace),
         out_shape=(
             jax.ShapeDtypeStruct((depth, yq, cols), F32),
@@ -450,12 +524,17 @@
             field,
             jax.ShapeDtypeStruct((8, 128), F32),
         ),
-        in_specs=[smem, smem, smem, anyspace, anyspace] + [vmem] * 6,
+        in_specs=[smem] * 4 + [anyspace] * 4 + [vmem] * 2,
         out_specs=(vmem, anyspace, anyspace, vmem),
         scratch_shapes=[
             pltpu.VMEM((ITERS + 2, depth + 2 * W, rows, cols), F32),
             pltpu.VMEM((ITERS - 1, depth, rows, cols), F32),
-            pltpu.VMEM((depth, rows, 128), F32),
+            pltpu.VMEM((depth, rows, cols), F32),
+            pltpu.VMEM((levels, depth, rows, QBLOCK), jnp.int32),
+            pltpu.VMEM((128 // depth, depth, rows * blocks), F32),
+            pltpu.VMEM((blocks, rows, 128), F32),
+            pltpu.VMEM((nrec, 128), jnp.int32),
+            pltpu.VMEM((ITERS, nrec, 128), F32),
             pltpu.VMEM((depth, rows, cols), F32),
             pltpu.VMEM((pairs, depth, yq, cols), F32),
             pltpu.VMEM((pairs, depth, yq, cols), F32),
@@ -466,7 +545,7 @@
             pltpu.VMEM((cols, cols), BF16),
             pltpu.VMEM((cols, cols), BF16),
             pltpu.VMEM((ITERS, nrec, QBLOCK), jnp.int32),
-            pltpu.VMEM((nrec, 128), F32),
+            pltpu.VMEM((ITERS, nrec, rows * blocks), F32),
             pltpu.VMEM((nshot, 8, 128), F32),
             pltpu.VMEM((nspace, 8, 128), F32),
             pltpu.VMEM((8, 128), F32),
@@ -481,7 +560,7 @@
             dma((nshot - 1,)),
             dma((nspace - 1,)),
             dma((nspace - 1,)),
-            dma((4,)),
+            dma((8,)),
         ],
         compiler_params=pltpu.CompilerParams(
             collective_id=0, has_side_effects=True, vmem_limit_bytes=66000000
@@ -490,17 +569,29 @@
         receiver_cell[0],
         source_cell[0],
         scale_table,
+        observed[0],
         adjoint_now[0],
         adjoint_later[0],
         courant,
         checkpoint_codes[0],
-        index,
+        scale_index[0],
         receiver_cell,
-        receiver_cell.reshape(nrec, 1),
-        observed[0].T,
     )
     count = nshot * ITERS * nrec * nspace
-    return (gradient, first[None], second[None], 0.5 * misfit[0, 0] / count)
+    parts = depth // W
+    gradient, first, second, misfit = pl.pallas_call(
+        functools.partial(finish, 0.5 / count),
+        out_shape=(jax.ShapeDtypeStruct(gradient.shape, F32), field, field, jax.ShapeDtypeStruct((1, 1), F32)),
+        in_specs=[anyspace] * 3 + [vmem],
+        out_specs=(anyspace, anyspace, anyspace, vmem),
+        scratch_shapes=[
+            pltpu.VMEM((depth, yq, cols), F32),
+            pltpu.VMEM((2 * parts, W, rows, cols), F32),
+            dma((2 * parts + 1,)),
+            dma((2 * parts + 1,)),
+        ],
+    )(gradient, first, second, total)
+    return (gradient, first[None], second[None], misfit.reshape(()))
 
 
 def solution(mesh):

time: 128 us -> 111 us (0.87)
  local copies, waits for them, and re-layouts: 13.1 us -> 0 us
  Pallas kernels: 112 us -> 110 us
  between operations: 2.44 us -> 0.64 us
    unnamed x7 -> x0, local copies, waits for them, and re-layouts: 9.13 us -> none
    pallas_call x1, Pallas kernels: 112 us -> 104 us  [body(): pl.pallas_call(functools.partial(kernel, nshot, nspace), out_shape=(jax.S...]
    pallas_call x0 -> x1, Pallas kernels: none -> 5.34 us  [body(): pl.pallas_call(functools.partial(finish, 0.5 / count), out_shape=(jax.Sha...]
    reshape x2 -> x0, local copies, waits for them, and re-layouts: 1.71 us -> none  [the longest x1 1.47 us: body(): receiver_cell.reshape(nrec, 1)]
where the time goes in v2:
time: 111 us; the launch traced here: 110 us
  Pallas kernels  110 us (99%)
    pallas_call x1, Pallas kernels, body(): pl.pallas_call(functools.partial(kernel, nshot, nspace), out_shape=(jax.S...  104 us
    pallas_call x1, Pallas kernels, body(): pl.pallas_call(functools.partial(finish, 0.5 / count), out_shape=(jax.Sha...  5.34 us

profile of v2, /device:TPU:2, one launch (start us, length us, event | category | flops | bytes accessed | tf_op | source)
XLA Modules:
  0.0 110.4 jit_solution(3049685303588755016)
XLA Ops:
  0.6 104.4 %shard_map.120 = (f32[16,16,512]{2,1,0:T(8,128)}, f32[16,64,512]{2,1,0:T(8,128)}, f32[16,64,512]{2,1,0:T(8,128)}, f32[8,128]{1,0:T(8,128)}) custom-call(s32[256]{0:T(256)} %bitcast.15, s32[3]{0:T(128)} %bitcast.16, f32[64]{0:T(128)} %table.1, f32[4,256]{1,0:T(4,128)} %bitcast.14, f32[16,64,512]{2,1,0:T(8,128)} %bitcast.11, f32[16,64,512]{2,1,0:T(8,128)} %bitcast.12, ...), custom_call_target="tpu_custom_call" | custom-call | tf_op jit(solution)/shard_map/pallas_call | solution.py:519
  105.0 5.3 %shard_map.121 = (f32[16,16,512]{2,1,0:T(8,128)}, f32[16,64,512]{2,1,0:T(8,128)}, f32[16,64,512]{2,1,0:T(8,128)}, f32[1,1]{1,0:T(1,128)}) custom-call(f32[16,16,512]{2,1,0:T(8,128)} %get-tuple-element.12.grad, f32[16,64,512]{2,1,0:T(8,128)} %get-tuple-element.13.first, f32[16,64,512]{2,1,0:T(8,128)} %get-tuple-element.14.second, ...), custom_call_target="tpu_custom_call" | custom-call | tf_op jit(solution)/shard_map/pallas_call | solution.py:582
